TPU v7x, 128 devices: a whole 4x4x4 slice. The times are simulated.
128 devices in a mesh: dp: 8 (over x, core), pipe: 4 (over y), tensor: 4 (over z).
Axes of the slice: x: 4, y: 4, z: 4, core: 2. Of those that a mesh axis runs over, the one named last changes fastest.
Arguments:
- support_tokens: int32 [64, 32], P(('dp', 'pipe')), may hold values from 0 to 64127
- support_lengths: int32 [64], P(('dp', 'pipe')), may hold values from 1 to 32
- support_labels: int32 [64, 1], P(('dp', 'pipe')), may hold values from 0 to 31
- query_tokens: int32 [32, 32], P(('dp', 'pipe')), may hold values from 0 to 64127
- query_lengths: int32 [32], P(('dp', 'pipe')), may hold values from 1 to 32
- query_episodes: int32 [32], P(('dp', 'pipe')), may hold values from 0 to 1
- embedding: bfloat16 [64128, 4096], P(('dp', 'pipe'), 'tensor'), may hold values from -18 to 18
- attn_gain: float32 [4, 4096], P('pipe'), may hold values from 0.5 to 1.5
- query_weight: bfloat16 [4, 4096, 4096], P('pipe', None, 'tensor'), may hold values from -1 to 1
- key_weight: bfloat16 [4, 4096, 1024], P('pipe', None, 'tensor'), may hold values from -16 to 16
- value_weight: bfloat16 [4, 4096, 1024], P('pipe', None, 'tensor'), may hold values from -0.09375 to 0.09375
- out_weight: bfloat16 [4, 4096, 4096], P('pipe', 'tensor'), may hold values from -0.09375 to 0.09375
- final_gain: float32 [4096], replicated, may hold values from 0.5 to 1.5
Outputs:
- prototypes: float32 [32, 4096], P(None, 'tensor')
- logits: float32 [32, 16], P(('dp', 'pipe'))
Inputs may be any that keep to these rules, and one draw needn't show every extreme that they name: `support_labels`: every class is the label of at least one support sequence.
All inputs are finite; a program needn't handle non-finite values.
Results may differ from a plain program's by a relative error of at most 0.024.
Values may be sent and summed in bfloat16 or wider, within the bound.
A program may use at most 128 MiB of HBM per device.

v0:
```python
import math
import jax
import jax.numpy as jnp
from jax import lax
from jax.sharding import PartitionSpec as P

D = 4096
HEAD_DIM = 128
WAYS = 16
EPISODES = 2
epsilon = 1e-05
rotary_base = 500000.0


def in_order(blocks, dim):
    blocks = jnp.moveaxis(blocks, 0, dim)
    dims = blocks.shape
    return blocks.reshape(*dims[:dim], dims[dim] * dims[dim + 1], *dims[dim + 2 :])


def sent_to_all(shard, axis):
    copies = jnp.broadcast_to(shard, (lax.axis_size(axis), *shard.shape))
    return lax.all_to_all(copies, axis, split_axis=0, concat_axis=0, tiled=True)


def collect(shard, axis, dim):
    return in_order(sent_to_all(shard, axis), dim)


def split_up(shard, dim, length):
    dims = shard.shape
    blocks = shard.reshape(*dims[:dim], length, dims[dim] // length, *dims[dim + 1 :])
    return jnp.moveaxis(blocks, dim, 0)


def sum_at_owner(shard, axis, dim):
    length = lax.axis_size(axis)
    blocks = lax.all_to_all(split_up(shard, dim, length), axis, 0, 0, tiled=True)
    return jnp.sum(blocks.astype(jnp.float32), axis=0)


def passed_along(block, axis, distance):
    devices = range(lax.axis_size(axis))
    route = [((i - distance) % len(devices), i) for i in devices]
    return lax.ppermute(block, axis, route)


def over_copies(shard, axis):
    return sent_to_all(shard, axis).astype(jnp.float32).sum(axis=0)


def rotate(heads_in, seq_len):
    half_dim = HEAD_DIM // 2
    freqs = jnp.exp(
        -math.log(rotary_base) * jnp.arange(half_dim, dtype=jnp.float32) * (2.0 / HEAD_DIM)
    )
    angles = jnp.arange(seq_len, dtype=jnp.float32)[:, None] * freqs[None, :]
    cosine = jnp.cos(angles)[None, :, None, :]
    sine = jnp.sin(angles)[None, :, None, :]
    first_half = heads_in[..., :half_dim]
    second_half = heads_in[..., half_dim:]
    return jnp.concatenate(
        [first_half * cosine - second_half * sine, second_half * cosine + first_half * sine],
        axis=-1,
    )


def whole_rows(hidden):
    return collect(hidden, "tensor", 1)


def whole_values(full_rows, gain_vector):
    values = full_rows.astype(jnp.float32)
    mean_square = jnp.mean(values * values, axis=-1, keepdims=True)
    return values * lax.rsqrt(mean_square + epsilon) * gain_vector


def shards(
    support_tokens,
    support_lengths,
    support_labels,
    query_tokens,
    query_lengths,
    query_episodes,
    embedding,
    attn_gain,
    query_weight,
    key_weight,
    value_weight,
    out_weight,
    final_gain,
):
    group_count = lax.axis_size(("dp", "pipe"))
    sections = lax.axis_size("pipe")
    sup_dev, seq_len = support_tokens.shape
    qry_dev = query_tokens.shape[0]
    seq_count = sup_dev + qry_dev
    row_count = seq_count * seq_len
    table_rows, width = embedding.shape
    column_start = lax.axis_index("tensor") * width
    all_support, all_query, every_sup_len, every_qry_len = (
        lax.all_gather(support_tokens, ("dp", "pipe"), axis=0, tiled=True),
        lax.all_gather(query_tokens, ("dp", "pipe"), axis=0, tiled=True),
        lax.all_gather(support_lengths, ("dp", "pipe"), axis=0, tiled=True),
        lax.all_gather(query_lengths, ("dp", "pipe"), axis=0, tiled=True),
    )
    token_flat = jnp.concatenate(
        [all_support.reshape(group_count, sup_dev * seq_len), all_query], axis=1
    ).reshape(group_count * row_count)
    local_ids = token_flat - lax.axis_index(("dp", "pipe")) * table_rows
    inside = (local_ids >= 0) & (local_ids < table_rows)
    picked = jnp.take(embedding, jnp.clip(local_ids, 0, table_rows - 1), axis=0)
    picked = jnp.where(inside[:, None], picked, jnp.zeros_like(picked))
    replies = lax.all_to_all(picked, ("dp", "pipe"), split_axis=0, concat_axis=0, tiled=True)
    hidden = jnp.sum(
        replies.reshape(group_count, row_count, width).astype(jnp.float32), axis=0
    ).astype(jnp.bfloat16)
    seq_lengths = jnp.concatenate([support_lengths, query_lengths], axis=0)
    query_proj = query_weight[0]
    key_proj = key_weight[0]
    value_proj = value_weight[0]
    out_proj = out_weight[0]
    gain_vector = attn_gain[0]
    local_heads = query_proj.shape[1] // HEAD_DIM
    local_groups = key_proj.shape[1] // HEAD_DIM
    group_size = local_heads // local_groups
    w_in = jnp.concatenate([query_proj, key_proj, value_proj], axis=1)
    query_cols = local_heads * HEAD_DIM
    key_cols = local_groups * HEAD_DIM
    positions = jnp.arange(seq_len)
    causal = positions[None, :] <= positions[:, None]

    def section_block(stream, lengths_here):
        normed = whole_values(whole_rows(stream), gain_vector).astype(jnp.bfloat16)
        projected = jnp.dot(normed, w_in, preferred_element_type=jnp.float32)
        query_heads = projected[:, :query_cols].reshape(seq_count, seq_len, local_heads, HEAD_DIM)
        key_heads = projected[:, query_cols : query_cols + key_cols].reshape(
            seq_count, seq_len, local_groups, HEAD_DIM
        )
        value_heads = (
            projected[:, query_cols + key_cols :]
            .reshape(seq_count, seq_len, local_groups, HEAD_DIM)
            .astype(jnp.bfloat16)
        )
        query_heads = (
            rotate(query_heads, seq_len)
            .astype(jnp.bfloat16)
            .reshape(seq_count, seq_len, local_groups, group_size, HEAD_DIM)
        )
        key_heads = rotate(key_heads, seq_len).astype(jnp.bfloat16)
        scores = jnp.einsum(
            "sikgd,sjkd->skgij", query_heads, key_heads, preferred_element_type=jnp.float32
        ) / math.sqrt(HEAD_DIM)
        visible = causal[None, :, :] & (positions[None, None, :] < lengths_here[:, None, None])
        scores = jnp.where(visible[:, None, None, :, :], scores, -1e30)
        weights = jax.nn.softmax(scores, axis=-1).astype(jnp.bfloat16)
        mixed = jnp.einsum(
            "skgij,sjkd->sikgd", weights, value_heads, preferred_element_type=jnp.float32
        )
        mixed = mixed.astype(jnp.bfloat16).reshape(row_count, query_cols)
        partial_out = jnp.dot(mixed, out_proj, preferred_element_type=jnp.float32)
        summed = sum_at_owner(partial_out.astype(jnp.bfloat16), "tensor", 1)
        return (stream.astype(jnp.float32) + summed).astype(jnp.bfloat16)

    section_index = lax.axis_index("pipe")
    dp_base = lax.axis_index("dp") * sections

    def tick(tick_index, stream):
        held_group = dp_base + (section_index - tick_index) % sections
        sup_part = lax.dynamic_slice_in_dim(every_sup_len, held_group * sup_dev, sup_dev)
        qry_part = lax.dynamic_slice_in_dim(every_qry_len, held_group * qry_dev, qry_dev)
        lengths_here = jnp.concatenate([sup_part, qry_part], axis=0)
        first_tick = (tick_index - section_index) % sections
        active = (first_tick <= tick_index) & (tick_index < first_tick + sections)
        computed = section_block(stream, lengths_here)
        stream = jnp.where(active, computed, stream)
        return passed_along(stream, "pipe", 1)

    hidden = lax.fori_loop(0, 2 * sections, tick, hidden)
    final = lax.dynamic_slice_in_dim(
        whole_values(whole_rows(hidden), final_gain), column_start, width, 1
    )
    live = (positions[None, :] < seq_lengths[:, None]).astype(jnp.float32)
    pooled = jnp.sum(
        final.reshape(seq_count, seq_len, width) * live[:, :, None], axis=1
    ) / seq_lengths[:, None].astype(jnp.float32)
    support_pooled = pooled[:sup_dev]
    query_pooled = pooled[sup_dev:]
    class_count_all = EPISODES * WAYS
    onehot = (support_labels[:, 0][:, None] == jnp.arange(class_count_all)[None, :]).astype(
        jnp.float32
    )
    class_total = jnp.dot(onehot.T, support_pooled, precision=lax.Precision.HIGHEST)
    class_count = jnp.sum(onehot, axis=0)
    class_total, class_count = (
        over_copies(class_total.astype(jnp.bfloat16), ("dp", "pipe")).astype(jnp.float32),
        over_copies(class_count.astype(jnp.bfloat16), ("dp", "pipe")).astype(jnp.float32),
    )
    prototypes = class_total / class_count[:, None]
    episode_pick = (query_episodes[:, None] == jnp.arange(EPISODES)[None, :]).astype(jnp.float32)
    chosen = jnp.einsum(
        "qe,ewc->qwc",
        episode_pick,
        prototypes.reshape(EPISODES, WAYS, width),
        precision=lax.Precision.HIGHEST,
    )
    partial_distance = jnp.sum((query_pooled[:, None, :] - chosen) ** 2, axis=-1)
    distance = lax.psum(partial_distance, "tensor")
    logits = -distance / math.sqrt(D)
    return (prototypes, logits)


def solution(mesh):
    return jax.shard_map(
        shards,
        mesh=mesh,
        in_specs=(
            P(("dp", "pipe"), None),
            P(("dp", "pipe")),
            P(("dp", "pipe"), None),
            P(("dp", "pipe"), None),
            P(("dp", "pipe")),
            P(("dp", "pipe")),
            P(("dp", "pipe"), "tensor"),
            P("pipe", None),
            P("pipe", None, "tensor"),
            P("pipe", None, "tensor"),
            P("pipe", None, "tensor"),
            P("pipe", "tensor", None),
            P(),
        ),
        out_specs=(P(None, "tensor"), P(("dp", "pipe"), None)),
        check_vma=False,
    )
```

profile of v0, /device:TPU:0, one launch (start us, length us, event | category | flops | bytes accessed | tf_op | source)
XLA Modules:
  0.0 681.9 jit_solution(12424556584828293104)
XLA Ops:
  0.6 33.8 %all-gather.1 = s32[32,1,32]{2,1,0:T(1,128)S(1)} all-gather(s32[1,1,32]{2,1,0:T(1,128)} %bitcast.148), channel_id=1, replica_groups=mesh['dp'=8,'pipe'=4,'tensor'=4] {'dp','pipe'}, dimensions={0}, use_global_device_ids=true | all-gather | bytes 4224 | tf_op jit(solution)/shard_map/all_gather | solution.py:103
  34.4 36.5 %all-gather = s32[32,2,32]{2,1,0:T(2,128)S(1)} all-gather(s32[1,2,32]{2,1,0:T(2,128)} %bitcast.144), channel_id=1, replica_groups=mesh['dp'=8,'pipe'=4,'tensor'=4] {'dp','pipe'}, dimensions={0}, use_global_device_ids=true | all-gather | bytes 8448 | tf_op jit(solution)/shard_map/all_gather | solution.py:102
  71.2 18.7 %gather_fusion = bf16[3072,1024]{1,0:T(8,128)(2,1)} fusion(bf16[2004,1024]{1,0:T(8,128)(2,1)} %param.21, s32[3072]{0:T(1024)S(1)} %broadcast_clamp_fusion.1), kind=kCustom, calls=%fused_computation | custom fusion | bytes 12595200 | tf_op jit(solution)/shard_map/jit(_take)/gather | solution.py:112
  89.9 7.0 %select_select_fusion = bf16[32,96,1024]{2,1,0:T(8,128)(2,1)} fusion(bf16[32,96,1024]{2,1,0:T(8,128)(2,1)} %bitcast.128, pred[32,96]{1,0:T(8,128)(4,1)S(1)} %get-tuple-element.312, pred[32,96]{1,0:T(8,128)(4,1)S(1)} %get-tuple-element.322), kind=kLoop, calls=%fused_computation.56 | loop fusion | flops 6291456 | bytes 12589056 | tf_op jit(solution)/shard_map/jit(_where)/select_n | solution.py:113
  96.9 5.7 all-to-all-start.2
  105.7 79.5 %all-reduce.2 = (s32[64]{0:T(128)S(1)}, s32[32]{0:T(128)S(1)}) all-reduce(s32[64]{0:T(128)S(1)} %dynamic-update-slice, s32[32]{0:T(128)S(1)} %dynamic-update-slice.1), channel_id=1, replica_groups=mesh['dp'=8,'pipe'=4,'tensor'=4] {'dp','pipe'}, use_global_device_ids=true, to_apply=%add | all-reduce | flops 96 | bytes 768
  185.3 11.6 %pad_maximum_fusion = bf16[4096,1536]{1,0:T(8,128)(2,1)} fusion(bf16[4096,256]{1,0:T(8,128)(2,1)S(1)} %bitcast.135, bf16[4096,256]{1,0:T(8,128)(2,1)} %bitcast.136, bf16[4096,1024]{1,0:T(8,128)(2,1)} %bitcast.129), kind=kLoop, calls=%fused_computation.55 | loop fusion | flops 37748736 | bytes 25165824 | tf_op jit(solution)/shard_map/concatenate | solution.py:127
  196.8 4.3 reduce_sum.116
  201.1 409.0 %while.16 = (s32[]{:T(128)}, bf16[96,1024]{1,0:T(8,128)(2,1)S(1)}, s32[]{:T(128)}, f32[1,4096]{1,0:T(1,128)S(1)}, bf16[4096,1536]{1,0:T(8,128)(2,1)}, /*index=5*...) while((s32[]{:T(128)}, bf16[96,1024]{1,0:T(8,128)(2,1)S(1)}, ...), condition=%wide.region_6.7_spmd.clone, body=%wide.region_1.0_spmd.clone.sunk | while | flops 2038168704 | bytes 45535072 | solution.py:179
  202.2 5.3 all-to-all-start
  209.2 10.1 %all-to-all-done = bf16[4,96,1024]{2,1,0:T(8,128)(2,1)S(1)} async-done(((bf16[4,96,1024]{2,1,0:T(8,128)(2,1)}), bf16[4,96,1024]{2,1,0:T(8,128)(2,1)S(1)}, u32[]{:S(2)}, u32[]{:S(2)}) %all-to-all-start) | async-done | bytes 786464 | tf_op jit(solution)/shard_map/while/body/eval_jaxpr/all_to_all | solution.py:23
  219.9 6.8 fusion.84
  229.0 4.8 convolution_convert_fusion.4
  234.8 3.5 all-to-all-start.1
  238.3 11.0 %all-to-all-done.1 = bf16[4,96,1024]{2,1,0:T(8,128)(2,1)S(1)} async-done(((bf16[4,96,1024]{2,1,0:T(8,128)(2,1)}), bf16[4,96,1024]{2,1,0:T(8,128)(2,1)S(1)}, u32[]{:S(2)}, u32[]{:S(2)}) %all-to-all-start.1) | async-done | bytes 786464 | tf_op jit(solution)/shard_map/while/body/eval_jaxpr/all_to_all | solution.py:38
  250.6 5.8 collective-permute-done
  262.7 7.7 %all-to-all-done = bf16[4,96,1024]{2,1,0:T(8,128)(2,1)S(1)} async-done(((bf16[4,96,1024]{2,1,0:T(8,128)(2,1)}), bf16[4,96,1024]{2,1,0:T(8,128)(2,1)S(1)}, u32[]{:S(2)}, u32[]{:S(2)}) %all-to-all-start) | async-done | bytes 786464 | tf_op jit(solution)/shard_map/while/body/eval_jaxpr/all_to_all | solution.py:23
  271.0 6.8 fusion.84
  280.0 4.8 convolution_convert_fusion.4
  285.8 3.5 all-to-all-start.1
  289.3 9.4 %all-to-all-done.1 = bf16[4,96,1024]{2,1,0:T(8,128)(2,1)S(1)} async-done(((bf16[4,96,1024]{2,1,0:T(8,128)(2,1)}), bf16[4,96,1024]{2,1,0:T(8,128)(2,1)S(1)}, u32[]{:S(2)}, u32[]{:S(2)}) %all-to-all-start.1) | async-done | bytes 786464 | tf_op jit(solution)/shard_map/while/body/eval_jaxpr/all_to_all | solution.py:38
  299.0 6.9 %collective-permute-done = bf16[96,1024]{1,0:T(8,128)(2,1)S(1)} collective-permute-done((bf16[96,1024]{1,0:T(8,128)(2,1)S(1)}, bf16[96,1024]{1,0:T(8,128)(2,1)S(1)}, u32[]{:S(2)}, u32[]{:S(2)}) %collective-permute-start) | collective-permute-done | bytes 196640 | tf_op jit(solution)/shard_map/while/body/eval_jaxpr/ppermute | solution.py:45
  312.2 7.7 %all-to-all-done = bf16[4,96,1024]{2,1,0:T(8,128)(2,1)S(1)} async-done(((bf16[4,96,1024]{2,1,0:T(8,128)(2,1)}), bf16[4,96,1024]{2,1,0:T(8,128)(2,1)S(1)}, u32[]{:S(2)}, u32[]{:S(2)}) %all-to-all-start) | async-done | bytes 786464 | tf_op jit(solution)/shard_map/while/body/eval_jaxpr/all_to_all | solution.py:23
  320.4 6.8 fusion.84
  329.5 4.8 convolution_convert_fusion.4
  338.8 9.4 %all-to-all-done.1 = bf16[4,96,1024]{2,1,0:T(8,128)(2,1)S(1)} async-done(((bf16[4,96,1024]{2,1,0:T(8,128)(2,1)}), bf16[4,96,1024]{2,1,0:T(8,128)(2,1)S(1)}, u32[]{:S(2)}, u32[]{:S(2)}) %all-to-all-start.1) | async-done | bytes 786464 | tf_op jit(solution)/shard_map/while/body/eval_jaxpr/all_to_all | solution.py:38
  348.5 6.9 %collective-permute-done = bf16[96,1024]{1,0:T(8,128)(2,1)S(1)} collective-permute-done((bf16[96,1024]{1,0:T(8,128)(2,1)S(1)}, bf16[96,1024]{1,0:T(8,128)(2,1)S(1)}, u32[]{:S(2)}, u32[]{:S(2)}) %collective-permute-start) | collective-permute-done | bytes 196640 | tf_op jit(solution)/shard_map/while/body/eval_jaxpr/ppermute | solution.py:45
  356.4 3.5 all-to-all-start
  361.7 7.7 %all-to-all-done = bf16[4,96,1024]{2,1,0:T(8,128)(2,1)S(1)} async-done(((bf16[4,96,1024]{2,1,0:T(8,128)(2,1)}), bf16[4,96,1024]{2,1,0:T(8,128)(2,1)S(1)}, u32[]{:S(2)}, u32[]{:S(2)}) %all-to-all-start) | async-done | bytes 786464 | tf_op jit(solution)/shard_map/while/body/eval_jaxpr/all_to_all | solution.py:23
  369.9 6.8 fusion.84
  379.0 4.8 convolution_convert_fusion.4
  384.8 3.5 all-to-all-start.1
  388.3 9.4 %all-to-all-done.1 = bf16[4,96,1024]{2,1,0:T(8,128)(2,1)S(1)} async-done(((bf16[4,96,1024]{2,1,0:T(8,128)(2,1)}), bf16[4,96,1024]{2,1,0:T(8,128)(2,1)S(1)}, u32[]{:S(2)}, u32[]{:S(2)}) %all-to-all-start.1) | async-done | bytes 786464 | tf_op jit(solution)/shard_map/while/body/eval_jaxpr/all_to_all | solution.py:38
  398.0 6.9 %collective-permute-done = bf16[96,1024]{1,0:T(8,128)(2,1)S(1)} collective-permute-done((bf16[96,1024]{1,0:T(8,128)(2,1)S(1)}, bf16[96,1024]{1,0:T(8,128)(2,1)S(1)}, u32[]{:S(2)}, u32[]{:S(2)}) %collective-permute-start) | collective-permute-done | bytes 196640 | tf_op jit(solution)/shard_map/while/body/eval_jaxpr/ppermute | solution.py:45
  405.9 3.5 all-to-all-start
  411.2 7.7 %all-to-all-done = bf16[4,96,1024]{2,1,0:T(8,128)(2,1)S(1)} async-done(((bf16[4,96,1024]{2,1,0:T(8,128)(2,1)}), bf16[4,96,1024]{2,1,0:T(8,128)(2,1)S(1)}, u32[]{:S(2)}, u32[]{:S(2)}) %all-to-all-start) | async-done | bytes 786464 | tf_op jit(solution)/shard_map/while/body/eval_jaxpr/all_to_all | solution.py:23
  419.4 6.8 fusion.84
  428.5 4.8 convolution_convert_fusion.4
  434.3 3.5 all-to-all-start.1
  437.8 10.7 %all-to-all-done.1 = bf16[4,96,1024]{2,1,0:T(8,128)(2,1)S(1)} async-done(((bf16[4,96,1024]{2,1,0:T(8,128)(2,1)}), bf16[4,96,1024]{2,1,0:T(8,128)(2,1)S(1)}, u32[]{:S(2)}, u32[]{:S(2)}) %all-to-all-start.1) | async-done | bytes 786464 | tf_op jit(solution)/shard_map/while/body/eval_jaxpr/all_to_all | solution.py:38
  448.8 6.9 %collective-permute-done = bf16[96,1024]{1,0:T(8,128)(2,1)S(1)} collective-permute-done((bf16[96,1024]{1,0:T(8,128)(2,1)S(1)}, bf16[96,1024]{1,0:T(8,128)(2,1)S(1)}, u32[]{:S(2)}, u32[]{:S(2)}) %collective-permute-start) | collective-permute-done | bytes 196640 | tf_op jit(solution)/shard_map/while/body/eval_jaxpr/ppermute | solution.py:45
  456.7 3.5 all-to-all-start
  462.0 7.7 %all-to-all-done = bf16[4,96,1024]{2,1,0:T(8,128)(2,1)S(1)} async-done(((bf16[4,96,1024]{2,1,0:T(8,128)(2,1)}), bf16[4,96,1024]{2,1,0:T(8,128)(2,1)S(1)}, u32[]{:S(2)}, u32[]{:S(2)}) %all-to-all-start) | async-done | bytes 786464 | tf_op jit(solution)/shard_map/while/body/eval_jaxpr/all_to_all | solution.py:23
  470.2 6.8 fusion.84
  479.2 4.8 convolution_convert_fusion.4
  485.0 3.5 all-to-all-start.1
  488.6 13.1 %all-to-all-done.1 = bf16[4,96,1024]{2,1,0:T(8,128)(2,1)S(1)} async-done(((bf16[4,96,1024]{2,1,0:T(8,128)(2,1)}), bf16[4,96,1024]{2,1,0:T(8,128)(2,1)S(1)}, u32[]{:S(2)}, u32[]{:S(2)}) %all-to-all-start.1) | async-done | bytes 786464 | tf_op jit(solution)/shard_map/while/body/eval_jaxpr/all_to_all | solution.py:38
  502.0 6.9 %collective-permute-done = bf16[96,1024]{1,0:T(8,128)(2,1)S(1)} collective-permute-done((bf16[96,1024]{1,0:T(8,128)(2,1)S(1)}, bf16[96,1024]{1,0:T(8,128)(2,1)S(1)}, u32[]{:S(2)}, u32[]{:S(2)}) %collective-permute-start) | collective-permute-done | bytes 196640 | tf_op jit(solution)/shard_map/while/body/eval_jaxpr/ppermute | solution.py:45
  515.1 7.7 %all-to-all-done = bf16[4,96,1024]{2,1,0:T(8,128)(2,1)S(1)} async-done(((bf16[4,96,1024]{2,1,0:T(8,128)(2,1)}), bf16[4,96,1024]{2,1,0:T(8,128)(2,1)S(1)}, u32[]{:S(2)}, u32[]{:S(2)}) %all-to-all-start) | async-done | bytes 786464 | tf_op jit(solution)/shard_map/while/body/eval_jaxpr/all_to_all | solution.py:23
  523.4 6.8 fusion.84
  532.4 4.8 convolution_convert_fusion.4
  541.8 10.0 %all-to-all-done.1 = bf16[4,96,1024]{2,1,0:T(8,128)(2,1)S(1)} async-done(((bf16[4,96,1024]{2,1,0:T(8,128)(2,1)}), bf16[4,96,1024]{2,1,0:T(8,128)(2,1)S(1)}, u32[]{:S(2)}, u32[]{:S(2)}) %all-to-all-start.1) | async-done | bytes 786464 | tf_op jit(solution)/shard_map/while/body/eval_jaxpr/all_to_all | solution.py:38
  552.0 6.9 %collective-permute-done = bf16[96,1024]{1,0:T(8,128)(2,1)S(1)} collective-permute-done((bf16[96,1024]{1,0:T(8,128)(2,1)S(1)}, bf16[96,1024]{1,0:T(8,128)(2,1)S(1)}, u32[]{:S(2)}, u32[]{:S(2)}) %collective-permute-start) | collective-permute-done | bytes 196640 | tf_op jit(solution)/shard_map/while/body/eval_jaxpr/ppermute | solution.py:45
  565.2 9.5 %all-to-all-done = bf16[4,96,1024]{2,1,0:T(8,128)(2,1)S(1)} async-done(((bf16[4,96,1024]{2,1,0:T(8,128)(2,1)}), bf16[4,96,1024]{2,1,0:T(8,128)(2,1)S(1)}, u32[]{:S(2)}, u32[]{:S(2)}) %all-to-all-start) | async-done | bytes 786464 | tf_op jit(solution)/shard_map/while/body/eval_jaxpr/all_to_all | solution.py:23
  575.2 6.8 fusion.84
  584.2 4.8 convolution_convert_fusion.4
  593.6 9.4 %all-to-all-done.1 = bf16[4,96,1024]{2,1,0:T(8,128)(2,1)S(1)} async-done(((bf16[4,96,1024]{2,1,0:T(8,128)(2,1)}), bf16[4,96,1024]{2,1,0:T(8,128)(2,1)S(1)}, u32[]{:S(2)}, u32[]{:S(2)}) %all-to-all-start.1) | async-done | bytes 786464 | tf_op jit(solution)/shard_map/while/body/eval_jaxpr/all_to_all | solution.py:38
  603.3 6.9 %collective-permute-done = bf16[96,1024]{1,0:T(8,128)(2,1)S(1)} collective-permute-done((bf16[96,1024]{1,0:T(8,128)(2,1)S(1)}, bf16[96,1024]{1,0:T(8,128)(2,1)S(1)}, u32[]{:S(2)}, u32[]{:S(2)}) %collective-permute-start) | collective-permute-done | bytes 196640 | tf_op jit(solution)/shard_map/while/body/eval_jaxpr/ppermute | solution.py:45
  614.9 9.2 %all-to-all-done.3 = bf16[4,96,1024]{2,1,0:T(8,128)(2,1)S(1)} async-done(((bf16[4,96,1024]{2,1,0:T(8,128)(2,1)}), bf16[4,96,1024]{2,1,0:T(8,128)(2,1)S(1)}, u32[]{:S(2)}, u32[]{:S(2)}) %all-to-all-start.3) | async-done | bytes 786464 | tf_op jit(solution)/shard_map/all_to_all | solution.py:23
  624.7 5.5 all-to-all-start.5
  631.5 6.0 all-to-all-done.5
  639.1 4.0 all-to-all-start.4
  643.8 27.6 %all-to-all-done.4 = bf16[32,32,1024]{2,1,0:T(8,128)(2,1)S(1)} async-done(((bf16[32,32,1024]{2,1,0:T(8,128)(2,1)}), bf16[32,32,1024]{2,1,0:T(8,128)(2,1)S(1)}, u32[]{:S(2)}, u32[]{:S(2)}) %all-to-all-start.4) | async-done | bytes 2097184 | tf_op jit(solution)/shard_map/all_to_all | solution.py:23
  672.4 8.9 %psum.7 = f32[1,16]{1,0:T(1,128)S(1)} all-reduce(f32[1,16]{1,0:T(1,128)S(1)} %bitcast.147), channel_id=1, replica_groups=mesh['dp'=8,'pipe'=4,'tensor'=4] {'tensor'}, use_global_device_ids=true, to_apply=%region_13.14 | all-reduce | flops 16 | bytes 128 | tf_op jit(solution)/shard_map/psum | solution.py:208
  (310 shorter events, 90.8 us)
Async XLA Ops:
  96.9 6.4 copy-start.5
  96.9 7.8 %copy-start.4 = (s32[2]{0:T(128)S(1)}, s32[2]{0:T(128)}, u32[]{:S(2)}) copy-start(s32[2]{0:T(128)} %param.16) | copy-start | bytes 28
  96.9 88.4 %copy-start = (bf16[1,4096,256]{2,1,0:T(8,128)(2,1)S(1)}, bf16[1,4096,256]{2,1,0:T(8,128)(2,1)}, u32[]{:S(2)}) copy-start(bf16[1,4096,256]{2,1,0:T(8,128)(2,1)} %param.25) | copy-start | bytes 6291460
  96.9 99.9 %all-to-all-start.2 = ((bf16[32,96,1024]{2,1,0:T(8,128)(2,1)}), bf16[32,96,1024]{2,1,0:T(8,128)(2,1)}, u32[]{:S(2)}, u32[]{:S(2)}) async-start(bf16[32,96,1024]{2,1,0:T(8,128)(2,1)} %select_select_fusion), calls=%async_computation.2 | async-start | bytes 12582912 | tf_op jit(solution)/shard_map/all_to_all | solution.py:114
  196.8 4.3 copy-start.1
  201.1 413.6 %copy-start.3 = (s32[2,1]{0,1:T(1,128)S(1)}, s32[2,1]{0,1:T(1,128)}, u32[]{:S(2)}) copy-start(s32[2,1]{0,1:T(1,128)} %param.17) | copy-start | bytes 28
  202.2 17.2 %all-to-all-start = ((bf16[4,96,1024]{2,1,0:T(8,128)(2,1)}), bf16[4,96,1024]{2,1,0:T(8,128)(2,1)S(1)}, u32[]{:S(2)}, u32[]{:S(2)}) async-start(bf16[4,96,1024]{2,1,0:T(8,128)(2,1)} %broadcast_in_dim.169), calls=%async_computation | async-start | bytes 1572864 | tf_op jit(solution)/shard_map/while/body/eval_jaxpr/all_to_all | solution.py:23
  234.8 14.5 %all-to-all-start.1 = ((bf16[4,96,1024]{2,1,0:T(8,128)(2,1)}), bf16[4,96,1024]{2,1,0:T(8,128)(2,1)S(1)}, u32[]{:S(2)}, u32[]{:S(2)}) async-start(bf16[4,96,1024]{2,1,0:T(8,128)(2,1)} %bitcast.122), calls=%async_computation.1 | async-start | bytes 1572864 | tf_op jit(solution)/shard_map/while/body/eval_jaxpr/all_to_all | solution.py:38
  249.5 6.9 %collective-permute-start = (bf16[96,1024]{1,0:T(8,128)(2,1)S(1)}, bf16[96,1024]{1,0:T(8,128)(2,1)S(1)}, u32[]{:S(2)}, u32[]{:S(2)}) collective-permute-start(bf16[96,1024]{1,0:T(8,128)(2,1)S(1)} %fusion.89), channel_id=1, source_target_pairs={{12,0},{0,4},{4,8},{8,12},{13,1},{1,5},{5,9},{9,13},{14,2},{2,6},{... | collective-permute-start | bytes 589832 | tf_op jit(solution)/shard_map/while/body/eval_jaxpr/ppermute | solution.py:45
  257.4 13.0 %all-to-all-start = ((bf16[4,96,1024]{2,1,0:T(8,128)(2,1)}), bf16[4,96,1024]{2,1,0:T(8,128)(2,1)S(1)}, u32[]{:S(2)}, u32[]{:S(2)}) async-start(bf16[4,96,1024]{2,1,0:T(8,128)(2,1)} %broadcast_in_dim.169), calls=%async_computation | async-start | bytes 1572864 | tf_op jit(solution)/shard_map/while/body/eval_jaxpr/all_to_all | solution.py:23
  285.8 13.0 %all-to-all-start.1 = ((bf16[4,96,1024]{2,1,0:T(8,128)(2,1)}), bf16[4,96,1024]{2,1,0:T(8,128)(2,1)S(1)}, u32[]{:S(2)}, u32[]{:S(2)}) async-start(bf16[4,96,1024]{2,1,0:T(8,128)(2,1)} %bitcast.122), calls=%async_computation.1 | async-start | bytes 1572864 | tf_op jit(solution)/shard_map/while/body/eval_jaxpr/all_to_all | solution.py:38
  299.0 6.9 %collective-permute-start = (bf16[96,1024]{1,0:T(8,128)(2,1)S(1)}, bf16[96,1024]{1,0:T(8,128)(2,1)S(1)}, u32[]{:S(2)}, u32[]{:S(2)}) collective-permute-start(bf16[96,1024]{1,0:T(8,128)(2,1)S(1)} %fusion.89), channel_id=1, source_target_pairs={{12,0},{0,4},{4,8},{8,12},{13,1},{1,5},{5,9},{9,13},{14,2},{2,6},{... | collective-permute-start | bytes 589832 | tf_op jit(solution)/shard_map/while/body/eval_jaxpr/ppermute | solution.py:45
  306.9 13.0 %all-to-all-start = ((bf16[4,96,1024]{2,1,0:T(8,128)(2,1)}), bf16[4,96,1024]{2,1,0:T(8,128)(2,1)S(1)}, u32[]{:S(2)}, u32[]{:S(2)}) async-start(bf16[4,96,1024]{2,1,0:T(8,128)(2,1)} %broadcast_in_dim.169), calls=%async_computation | async-start | bytes 1572864 | tf_op jit(solution)/shard_map/while/body/eval_jaxpr/all_to_all | solution.py:23
  335.3 13.0 %all-to-all-start.1 = ((bf16[4,96,1024]{2,1,0:T(8,128)(2,1)}), bf16[4,96,1024]{2,1,0:T(8,128)(2,1)S(1)}, u32[]{:S(2)}, u32[]{:S(2)}) async-start(bf16[4,96,1024]{2,1,0:T(8,128)(2,1)} %bitcast.122), calls=%async_computation.1 | async-start | bytes 1572864 | tf_op jit(solution)/shard_map/while/body/eval_jaxpr/all_to_all | solution.py:38
  348.5 6.9 %collective-permute-start = (bf16[96,1024]{1,0:T(8,128)(2,1)S(1)}, bf16[96,1024]{1,0:T(8,128)(2,1)S(1)}, u32[]{:S(2)}, u32[]{:S(2)}) collective-permute-start(bf16[96,1024]{1,0:T(8,128)(2,1)S(1)} %fusion.89), channel_id=1, source_target_pairs={{12,0},{0,4},{4,8},{8,12},{13,1},{1,5},{5,9},{9,13},{14,2},{2,6},{... | collective-permute-start | bytes 589832 | tf_op jit(solution)/shard_map/while/body/eval_jaxpr/ppermute | solution.py:45
  356.4 13.0 %all-to-all-start = ((bf16[4,96,1024]{2,1,0:T(8,128)(2,1)}), bf16[4,96,1024]{2,1,0:T(8,128)(2,1)S(1)}, u32[]{:S(2)}, u32[]{:S(2)}) async-start(bf16[4,96,1024]{2,1,0:T(8,128)(2,1)} %broadcast_in_dim.169), calls=%async_computation | async-start | bytes 1572864 | tf_op jit(solution)/shard_map/while/body/eval_jaxpr/all_to_all | solution.py:23
  384.8 13.0 %all-to-all-start.1 = ((bf16[4,96,1024]{2,1,0:T(8,128)(2,1)}), bf16[4,96,1024]{2,1,0:T(8,128)(2,1)S(1)}, u32[]{:S(2)}, u32[]{:S(2)}) async-start(bf16[4,96,1024]{2,1,0:T(8,128)(2,1)} %bitcast.122), calls=%async_computation.1 | async-start | bytes 1572864 | tf_op jit(solution)/shard_map/while/body/eval_jaxpr/all_to_all | solution.py:38
  397.9 6.9 %collective-permute-start = (bf16[96,1024]{1,0:T(8,128)(2,1)S(1)}, bf16[96,1024]{1,0:T(8,128)(2,1)S(1)}, u32[]{:S(2)}, u32[]{:S(2)}) collective-permute-start(bf16[96,1024]{1,0:T(8,128)(2,1)S(1)} %fusion.89), channel_id=1, source_target_pairs={{12,0},{0,4},{4,8},{8,12},{13,1},{1,5},{5,9},{9,13},{14,2},{2,6},{... | collective-permute-start | bytes 589832 | tf_op jit(solution)/shard_map/while/body/eval_jaxpr/ppermute | solution.py:45
  405.9 13.0 %all-to-all-start = ((bf16[4,96,1024]{2,1,0:T(8,128)(2,1)}), bf16[4,96,1024]{2,1,0:T(8,128)(2,1)S(1)}, u32[]{:S(2)}, u32[]{:S(2)}) async-start(bf16[4,96,1024]{2,1,0:T(8,128)(2,1)} %broadcast_in_dim.169), calls=%async_computation | async-start | bytes 1572864 | tf_op jit(solution)/shard_map/while/body/eval_jaxpr/all_to_all | solution.py:23
  434.3 14.2 %all-to-all-start.1 = ((bf16[4,96,1024]{2,1,0:T(8,128)(2,1)}), bf16[4,96,1024]{2,1,0:T(8,128)(2,1)S(1)}, u32[]{:S(2)}, u32[]{:S(2)}) async-start(bf16[4,96,1024]{2,1,0:T(8,128)(2,1)} %bitcast.122), calls=%async_computation.1 | async-start | bytes 1572864 | tf_op jit(solution)/shard_map/while/body/eval_jaxpr/all_to_all | solution.py:38
  448.7 6.9 %collective-permute-start = (bf16[96,1024]{1,0:T(8,128)(2,1)S(1)}, bf16[96,1024]{1,0:T(8,128)(2,1)S(1)}, u32[]{:S(2)}, u32[]{:S(2)}) collective-permute-start(bf16[96,1024]{1,0:T(8,128)(2,1)S(1)} %fusion.89), channel_id=1, source_target_pairs={{12,0},{0,4},{4,8},{8,12},{13,1},{1,5},{5,9},{9,13},{14,2},{2,6},{... | collective-permute-start | bytes 589832 | tf_op jit(solution)/shard_map/while/body/eval_jaxpr/ppermute | solution.py:45
  456.7 13.0 %all-to-all-start = ((bf16[4,96,1024]{2,1,0:T(8,128)(2,1)}), bf16[4,96,1024]{2,1,0:T(8,128)(2,1)S(1)}, u32[]{:S(2)}, u32[]{:S(2)}) async-start(bf16[4,96,1024]{2,1,0:T(8,128)(2,1)} %broadcast_in_dim.169), calls=%async_computation | async-start | bytes 1572864 | tf_op jit(solution)/shard_map/while/body/eval_jaxpr/all_to_all | solution.py:23
  485.0 16.7 %all-to-all-start.1 = ((bf16[4,96,1024]{2,1,0:T(8,128)(2,1)}), bf16[4,96,1024]{2,1,0:T(8,128)(2,1)S(1)}, u32[]{:S(2)}, u32[]{:S(2)}) async-start(bf16[4,96,1024]{2,1,0:T(8,128)(2,1)} %bitcast.122), calls=%async_computation.1 | async-start | bytes 1572864 | tf_op jit(solution)/shard_map/while/body/eval_jaxpr/all_to_all | solution.py:38
  501.9 6.9 %collective-permute-start = (bf16[96,1024]{1,0:T(8,128)(2,1)S(1)}, bf16[96,1024]{1,0:T(8,128)(2,1)S(1)}, u32[]{:S(2)}, u32[]{:S(2)}) collective-permute-start(bf16[96,1024]{1,0:T(8,128)(2,1)S(1)} %fusion.89), channel_id=1, source_target_pairs={{12,0},{0,4},{4,8},{8,12},{13,1},{1,5},{5,9},{9,13},{14,2},{2,6},{... | collective-permute-start | bytes 589832 | tf_op jit(solution)/shard_map/while/body/eval_jaxpr/ppermute | solution.py:45
  509.9 13.0 %all-to-all-start = ((bf16[4,96,1024]{2,1,0:T(8,128)(2,1)}), bf16[4,96,1024]{2,1,0:T(8,128)(2,1)S(1)}, u32[]{:S(2)}, u32[]{:S(2)}) async-start(bf16[4,96,1024]{2,1,0:T(8,128)(2,1)} %broadcast_in_dim.169), calls=%async_computation | async-start | bytes 1572864 | tf_op jit(solution)/shard_map/while/body/eval_jaxpr/all_to_all | solution.py:23
  538.2 13.5 %all-to-all-start.1 = ((bf16[4,96,1024]{2,1,0:T(8,128)(2,1)}), bf16[4,96,1024]{2,1,0:T(8,128)(2,1)S(1)}, u32[]{:S(2)}, u32[]{:S(2)}) async-start(bf16[4,96,1024]{2,1,0:T(8,128)(2,1)} %bitcast.122), calls=%async_computation.1 | async-start | bytes 1572864 | tf_op jit(solution)/shard_map/while/body/eval_jaxpr/all_to_all | solution.py:38
  551.9 6.9 %collective-permute-start = (bf16[96,1024]{1,0:T(8,128)(2,1)S(1)}, bf16[96,1024]{1,0:T(8,128)(2,1)S(1)}, u32[]{:S(2)}, u32[]{:S(2)}) collective-permute-start(bf16[96,1024]{1,0:T(8,128)(2,1)S(1)} %fusion.89), channel_id=1, source_target_pairs={{12,0},{0,4},{4,8},{8,12},{13,1},{1,5},{5,9},{9,13},{14,2},{2,6},{... | collective-permute-start | bytes 589832 | tf_op jit(solution)/shard_map/while/body/eval_jaxpr/ppermute | solution.py:45
  559.9 14.7 %all-to-all-start = ((bf16[4,96,1024]{2,1,0:T(8,128)(2,1)}), bf16[4,96,1024]{2,1,0:T(8,128)(2,1)S(1)}, u32[]{:S(2)}, u32[]{:S(2)}) async-start(bf16[4,96,1024]{2,1,0:T(8,128)(2,1)} %broadcast_in_dim.169), calls=%async_computation | async-start | bytes 1572864 | tf_op jit(solution)/shard_map/while/body/eval_jaxpr/all_to_all | solution.py:23
  590.0 13.0 %all-to-all-start.1 = ((bf16[4,96,1024]{2,1,0:T(8,128)(2,1)}), bf16[4,96,1024]{2,1,0:T(8,128)(2,1)S(1)}, u32[]{:S(2)}, u32[]{:S(2)}) async-start(bf16[4,96,1024]{2,1,0:T(8,128)(2,1)} %bitcast.122), calls=%async_computation.1 | async-start | bytes 1572864 | tf_op jit(solution)/shard_map/while/body/eval_jaxpr/all_to_all | solution.py:38
  603.2 6.9 %collective-permute-start = (bf16[96,1024]{1,0:T(8,128)(2,1)S(1)}, bf16[96,1024]{1,0:T(8,128)(2,1)S(1)}, u32[]{:S(2)}, u32[]{:S(2)}) collective-permute-start(bf16[96,1024]{1,0:T(8,128)(2,1)S(1)} %fusion.89), channel_id=1, source_target_pairs={{12,0},{0,4},{4,8},{8,12},{13,1},{1,5},{5,9},{9,13},{14,2},{2,6},{... | collective-permute-start | bytes 589832 | tf_op jit(solution)/shard_map/while/body/eval_jaxpr/ppermute | solution.py:45
  611.1 13.0 %all-to-all-start.3 = ((bf16[4,96,1024]{2,1,0:T(8,128)(2,1)}), bf16[4,96,1024]{2,1,0:T(8,128)(2,1)S(1)}, u32[]{:S(2)}, u32[]{:S(2)}) async-start(bf16[4,96,1024]{2,1,0:T(8,128)(2,1)} %broadcast_in_dim.128), calls=%async_computation.3 | async-start | bytes 1572864 | tf_op jit(solution)/shard_map/all_to_all | solution.py:23
  614.6 16.2 %dynamic-slice-start = ((f32[4096]{0:T(1024)}, s32[]{:T(128)}), f32[1024]{0:T(1024)S(1)}, s32[]{:S(2)}) async-start(f32[4096]{0:T(1024)} %param.27, s32[]{:T(128)} %select_n.118), calls=%async_computation.6 | async-start | bytes 8704 | tf_op jit(solution)/shard_map/dynamic_slice | solution.py:180
  624.7 12.8 %all-to-all-start.5 = ((bf16[32,1,32]{2,1,0:T(2,128)(2,1)}), bf16[32,1,32]{2,1,0:T(2,128)(2,1)S(1)}, u32[]{:S(2)}, u32[]{:S(2)}) async-start(bf16[32,1,32]{2,1,0:T(2,128)(2,1)} %broadcast_in_dim.130), calls=%async_computation.5 | async-start | bytes 32768 | tf_op jit(solution)/shard_map/all_to_all | solution.py:23
  639.1 32.3 %all-to-all-start.4 = ((bf16[32,32,1024]{2,1,0:T(8,128)(2,1)}), bf16[32,32,1024]{2,1,0:T(8,128)(2,1)S(1)}, u32[]{:S(2)}, u32[]{:S(2)}) async-start(bf16[32,32,1024]{2,1,0:T(8,128)(2,1)} %broadcast_in_dim.129), calls=%async_computation.4 | async-start | bytes 4194304 | tf_op jit(solution)/shard_map/all_to_all | solution.py:23
  671.9 10.0 %copy-start.2 = (f32[32,1024]{1,0:T(8,128)}, f32[32,1024]{1,0:T(8,128)S(1)}, u32[]{:S(2)}) copy-start(f32[32,1024]{1,0:T(8,128)S(1)} %broadcast_divide_fusion) | copy-start | bytes 393220
where the time goes:
time: 684 us; the launch traced here: 682 us
  waiting for transfers between devices  245 us (36%)
  blocking collectives  159 us (23%)
  matrix products  104 us (15%)
  starting transfers between devices  78.1 us (11%)
  local copies, waits for them, and re-layouts  51.8 us (8%)
  other arithmetic  39.9 us (6%)
    all_to_all x11, waiting for transfers between devices, sent_to_all(): return lax.all_to_all(copies, axis, split_axis=0, concat_axis=0, tiled=True)  108 us
    all_to_all x8, waiting for transfers between devices, sum_at_owner(): lax.all_to_all(split_up(shard, dim, length), axis, 0, 0, tiled=True)  82.5 us
    unnamed x1, blocking collectives  79.5 us
    dot_general x8, matrix products, section_block(): projected = jnp.dot(normed, w_in, preferred_element_type=jnp.float32)  54.2 us
    ppermute x8, waiting for transfers between devices, passed_along(): return lax.ppermute(block, axis, route)  53.9 us
    all_to_all x11, starting transfers between devices, sent_to_all(): return lax.all_to_all(copies, axis, split_axis=0, concat_axis=0, tiled=True)  42.8 us
    dot_general x8, matrix products, section_block(): partial_out = jnp.dot(mixed, out_proj, preferred_element_type=jnp.float32)  38.7 us
    all_gather x1, blocking collectives, shards(): lax.all_gather(support_tokens, ('dp', 'pipe'), axis=0, tiled=True)  36.5 us
  transfers between devices with their start and end apart: 28, of which 27 were waited for; matrix products, arithmetic and copies ran while one was open for 4% of the time, Pallas kernels for 0%

commit v1 on v0

--- a/solution.py
+++ b/solution.py
@@ -10,6 +10,35 @@
 EPISODES = 2
 epsilon = 1e-05
 rotary_base = 500000.0
+
+
+def follow_quotas(local_array, along_dim):
+    local_array = jnp.moveaxis(local_array, 0, along_dim)
+    side_arr = local_array.shape
+    return local_array.reshape(
+        *side_arr[:along_dim],
+        side_arr[along_dim] * side_arr[along_dim + 1],
+        *side_arr[along_dim + 2 :]
+    )
+
+
+def feed_set(buf, axis_name):
+    val2, view_out = (lax.axis_size(axis_name), lax.axis_index(axis_name))
+    newest, odd = (buf[None], 1)
+    while odd < val2:
+        taken_in = lax.ppermute(
+            newest, axis_name=axis_name, perm=tuple(((to_i, to_i ^ odd) for to_i in range(val2)))
+        )
+        x_new = view_out & odd == 0
+        newest = jnp.concatenate(
+            [jnp.where(x_new, newest, taken_in), jnp.where(x_new, taken_in, newest)]
+        )
+        odd *= 2
+    return newest
+
+
+def map_series_on(local_block, t0, at_axis):
+    return follow_quotas(feed_set(local_block, t0), at_axis)
 
 
 def in_order(blocks, dim):
@@ -99,7 +128,7 @@
     table_rows, width = embedding.shape
     column_start = lax.axis_index("tensor") * width
     all_support, all_query, every_sup_len, every_qry_len = (
-        lax.all_gather(support_tokens, ("dp", "pipe"), axis=0, tiled=True),
+        map_series_on(support_tokens, ("dp", "pipe"), at_axis=0),
         lax.all_gather(query_tokens, ("dp", "pipe"), axis=0, tiled=True),
         lax.all_gather(support_lengths, ("dp", "pipe"), axis=0, tiled=True),
         lax.all_gather(query_lengths, ("dp", "pipe"), axis=0, tiled=True),

time: 684 us -> 664 us (0.971)
  blocking collectives: 159 us -> 121 us
  starting transfers between devices: 78.1 us -> 87.5 us
  waiting for transfers between devices: 245 us -> 252 us
    all_gather x1 -> x0, blocking collectives: 36.5 us -> none  [shards(): lax.all_gather(support_tokens, ('dp', 'pipe'), axis=0, tiled=True)]
    ppermute x0 -> x5, starting transfers between devices: none -> 10.1 us  [feed_set(): lax.ppermute(newest, axis_name=axis_name, perm=tuple(((to_i, to_i ^ odd)...]
    ppermute x0 -> x5, waiting for transfers between devices: none -> 7.08 us  [feed_set(): lax.ppermute(newest, axis_name=axis_name, perm=tuple(((to_i, to_i ^ odd)...]
  transfers between devices with their start and end apart: 28 -> 33, of which waited for: 27 -> 31; matrix products, arithmetic and copies ran while one was open for 4% -> 4% of each run, Pallas kernels for 0% -> 0%
where the time goes in v1:
time: 664 us; the launch traced here: 662 us
  waiting for transfers between devices  252 us (38%)
  blocking collectives  121 us (18%)
  matrix products  104 us (16%)
  starting transfers between devices  87.5 us (13%)
  local copies, waits for them, and re-layouts  51.8 us (8%)
  other arithmetic  40.6 us (6%)
    all_to_all x11, waiting for transfers between devices, sent_to_all(): return lax.all_to_all(copies, axis, split_axis=0, concat_axis=0, tiled=True)  108 us
    all_to_all x8, waiting for transfers between devices, sum_at_owner(): lax.all_to_all(split_up(shard, dim, length), axis, 0, 0, tiled=True)  82.5 us
    unnamed x1, blocking collectives  79.4 us
    dot_general x8, matrix products, section_block(): projected = jnp.dot(normed, w_in, preferred_element_type=jnp.float32)  54.2 us
    ppermute x8, waiting for transfers between devices, passed_along(): return lax.ppermute(block, axis, route)  53.8 us
    all_to_all x11, starting transfers between devices, sent_to_all(): return lax.all_to_all(copies, axis, split_axis=0, concat_axis=0, tiled=True)  42.8 us
    dot_general x8, matrix products, section_block(): partial_out = jnp.dot(mixed, out_proj, preferred_element_type=jnp.float32)  38.7 us
    all_gather x1, blocking collectives, shards(): lax.all_gather(query_tokens, ('dp', 'pipe'), axis=0, tiled=True)  32.8 us
  transfers between devices with their start and end apart: 33, of which 31 were waited for; matrix products, arithmetic and copies ran while one was open for 4% of the time, Pallas kernels for 0%

profile of v1, /device:TPU:0, one launch (start us, length us, event | category | flops | bytes accessed | tf_op | source)
XLA Modules:
  0.0 661.5 jit_solution(6167167001249094937)
XLA Ops:
  18.5 32.8 %all-gather = s32[32,1,32]{2,1,0:T(1,128)S(1)} all-gather(s32[1,1,32]{2,1,0:T(1,128)} %bitcast.150), channel_id=1, replica_groups=mesh['dp'=8,'pipe'=4,'tensor'=4] {'dp','pipe'}, dimensions={0}, use_global_device_ids=true | all-gather | bytes 4224 | tf_op jit(solution)/shard_map/all_gather | solution.py:132
  51.7 18.7 %gather_fusion = bf16[3072,1024]{1,0:T(8,128)(2,1)} fusion(bf16[2004,1024]{1,0:T(8,128)(2,1)} %param.21, s32[3072]{0:T(1024)S(1)} %broadcast_clamp_fusion.1), kind=kCustom, calls=%fused_computation | custom fusion | bytes 12595200 | tf_op jit(solution)/shard_map/jit(_take)/gather | solution.py:141
  70.4 7.0 %select_select_fusion = bf16[32,96,1024]{2,1,0:T(8,128)(2,1)} fusion(bf16[32,96,1024]{2,1,0:T(8,128)(2,1)} %bitcast.130, pred[32,96]{1,0:T(8,128)(4,1)S(1)} %get-tuple-element.312, pred[32,96]{1,0:T(8,128)(4,1)S(1)} %get-tuple-element.322), kind=kLoop, calls=%fused_computation.56 | loop fusion | flops 6291456 | bytes 12589056 | tf_op jit(solution)/shard_map/jit(_where)/select_n | solution.py:142
  77.4 5.0 all-to-all-start.2
  85.5 79.4 %all-reduce.2 = (s32[64]{0:T(128)S(1)}, s32[32]{0:T(128)S(1)}) all-reduce(s32[64]{0:T(128)S(1)} %dynamic-update-slice, s32[32]{0:T(128)S(1)} %dynamic-update-slice.1), channel_id=1, replica_groups=mesh['dp'=8,'pipe'=4,'tensor'=4] {'dp','pipe'}, use_global_device_ids=true, to_apply=%add | all-reduce | flops 96 | bytes 768
  164.9 11.6 %pad_maximum_fusion = bf16[4096,1536]{1,0:T(8,128)(2,1)} fusion(bf16[4096,256]{1,0:T(8,128)(2,1)S(1)} %bitcast.137, bf16[4096,256]{1,0:T(8,128)(2,1)} %bitcast.138, bf16[4096,1024]{1,0:T(8,128)(2,1)} %bitcast.131), kind=kLoop, calls=%fused_computation.55 | loop fusion | flops 37748736 | bytes 25165824 | tf_op jit(solution)/shard_map/concatenate | solution.py:156
  176.5 4.3 reduce_sum.116
  180.8 409.0 %while.16 = (s32[]{:T(128)}, bf16[96,1024]{1,0:T(8,128)(2,1)S(1)}, s32[]{:T(128)}, f32[1,4096]{1,0:T(1,128)S(1)}, bf16[4096,1536]{1,0:T(8,128)(2,1)}, /*index=5*...) while((s32[]{:T(128)}, bf16[96,1024]{1,0:T(8,128)(2,1)S(1)}, ...), condition=%wide.region_6.7_spmd.clone, body=%wide.region_1.6_spmd.clone.sunk | while | flops 2038168704 | bytes 45535072 | solution.py:208
  181.8 5.3 all-to-all-start
  188.9 10.1 %all-to-all-done = bf16[4,96,1024]{2,1,0:T(8,128)(2,1)S(1)} async-done(((bf16[4,96,1024]{2,1,0:T(8,128)(2,1)}), bf16[4,96,1024]{2,1,0:T(8,128)(2,1)S(1)}, u32[]{:S(2)}, u32[]{:S(2)}) %all-to-all-start) | async-done | bytes 786464 | tf_op jit(solution)/shard_map/while/body/eval_jaxpr/all_to_all | solution.py:52
  199.6 6.8 %fusion.84 = f32[96,1536]{1,0:T(8,128)S(1)} fusion(bf16[4096,1536]{1,0:T(8,128)(2,1)} %get-tuple-element.440, f32[96,4096]{1,0:T(8,128)S(1)} %bitcast.127, f32[4096]{0:T(1024)S(1)} %bitcast.139, f32[96]{0:T(128)S(1)} %add_rsqrt_fusion.3), kind=kOutput, calls=%fused_computation.17.clone.1 | convolution fusion | flops 1209139200 | bytes 14762368 | tf_op jit(solution)/shard_map/while/body/eval_jaxpr/dot_general | solution.py:164
  208.6 4.8 convolution_convert_fusion.4
  214.4 3.5 all-to-all-start.1
  218.0 11.0 %all-to-all-done.1 = bf16[4,96,1024]{2,1,0:T(8,128)(2,1)S(1)} async-done(((bf16[4,96,1024]{2,1,0:T(8,128)(2,1)}), bf16[4,96,1024]{2,1,0:T(8,128)(2,1)S(1)}, u32[]{:S(2)}, u32[]{:S(2)}) %all-to-all-start.1) | async-done | bytes 786464 | tf_op jit(solution)/shard_map/while/body/eval_jaxpr/all_to_all | solution.py:67
  230.3 5.8 collective-permute-done
  237.1 3.5 all-to-all-start
  242.4 7.7 %all-to-all-done = bf16[4,96,1024]{2,1,0:T(8,128)(2,1)S(1)} async-done(((bf16[4,96,1024]{2,1,0:T(8,128)(2,1)}), bf16[4,96,1024]{2,1,0:T(8,128)(2,1)S(1)}, u32[]{:S(2)}, u32[]{:S(2)}) %all-to-all-start) | async-done | bytes 786464 | tf_op jit(solution)/shard_map/while/body/eval_jaxpr/all_to_all | solution.py:52
  250.6 6.8 %fusion.84 = f32[96,1536]{1,0:T(8,128)S(1)} fusion(bf16[4096,1536]{1,0:T(8,128)(2,1)} %get-tuple-element.440, f32[96,4096]{1,0:T(8,128)S(1)} %bitcast.127, f32[4096]{0:T(1024)S(1)} %bitcast.139, f32[96]{0:T(128)S(1)} %add_rsqrt_fusion.3), kind=kOutput, calls=%fused_computation.17.clone.1 | convolution fusion | flops 1209139200 | bytes 14762368 | tf_op jit(solution)/shard_map/while/body/eval_jaxpr/dot_general | solution.py:164
  259.6 4.8 convolution_convert_fusion.4
  265.5 3.5 all-to-all-start.1
  269.0 9.4 %all-to-all-done.1 = bf16[4,96,1024]{2,1,0:T(8,128)(2,1)S(1)} async-done(((bf16[4,96,1024]{2,1,0:T(8,128)(2,1)}), bf16[4,96,1024]{2,1,0:T(8,128)(2,1)S(1)}, u32[]{:S(2)}, u32[]{:S(2)}) %all-to-all-start.1) | async-done | bytes 786464 | tf_op jit(solution)/shard_map/while/body/eval_jaxpr/all_to_all | solution.py:67
  278.7 6.9 %collective-permute-done = bf16[96,1024]{1,0:T(8,128)(2,1)S(1)} collective-permute-done((bf16[96,1024]{1,0:T(8,128)(2,1)S(1)}, bf16[96,1024]{1,0:T(8,128)(2,1)S(1)}, u32[]{:S(2)}, u32[]{:S(2)}) %collective-permute-start) | collective-permute-done | bytes 196640 | tf_op jit(solution)/shard_map/while/body/eval_jaxpr/ppermute | solution.py:74
  291.9 7.7 %all-to-all-done = bf16[4,96,1024]{2,1,0:T(8,128)(2,1)S(1)} async-done(((bf16[4,96,1024]{2,1,0:T(8,128)(2,1)}), bf16[4,96,1024]{2,1,0:T(8,128)(2,1)S(1)}, u32[]{:S(2)}, u32[]{:S(2)}) %all-to-all-start) | async-done | bytes 786464 | tf_op jit(solution)/shard_map/while/body/eval_jaxpr/all_to_all | solution.py:52
  300.1 6.8 %fusion.84 = f32[96,1536]{1,0:T(8,128)S(1)} fusion(bf16[4096,1536]{1,0:T(8,128)(2,1)} %get-tuple-element.440, f32[96,4096]{1,0:T(8,128)S(1)} %bitcast.127, f32[4096]{0:T(1024)S(1)} %bitcast.139, f32[96]{0:T(128)S(1)} %add_rsqrt_fusion.3), kind=kOutput, calls=%fused_computation.17.clone.1 | convolution fusion | flops 1209139200 | bytes 14762368 | tf_op jit(solution)/shard_map/while/body/eval_jaxpr/dot_general | solution.py:164
  309.1 4.8 convolution_convert_fusion.4
  314.9 3.5 all-to-all-start.1
  318.5 9.4 %all-to-all-done.1 = bf16[4,96,1024]{2,1,0:T(8,128)(2,1)S(1)} async-done(((bf16[4,96,1024]{2,1,0:T(8,128)(2,1)}), bf16[4,96,1024]{2,1,0:T(8,128)(2,1)S(1)}, u32[]{:S(2)}, u32[]{:S(2)}) %all-to-all-start.1) | async-done | bytes 786464 | tf_op jit(solution)/shard_map/while/body/eval_jaxpr/all_to_all | solution.py:67
  328.2 6.9 %collective-permute-done = bf16[96,1024]{1,0:T(8,128)(2,1)S(1)} collective-permute-done((bf16[96,1024]{1,0:T(8,128)(2,1)S(1)}, bf16[96,1024]{1,0:T(8,128)(2,1)S(1)}, u32[]{:S(2)}, u32[]{:S(2)}) %collective-permute-start) | collective-permute-done | bytes 196640 | tf_op jit(solution)/shard_map/while/body/eval_jaxpr/ppermute | solution.py:74
  341.3 7.7 %all-to-all-done = bf16[4,96,1024]{2,1,0:T(8,128)(2,1)S(1)} async-done(((bf16[4,96,1024]{2,1,0:T(8,128)(2,1)}), bf16[4,96,1024]{2,1,0:T(8,128)(2,1)S(1)}, u32[]{:S(2)}, u32[]{:S(2)}) %all-to-all-start) | async-done | bytes 786464 | tf_op jit(solution)/shard_map/while/body/eval_jaxpr/all_to_all | solution.py:52
  349.6 6.8 %fusion.84 = f32[96,1536]{1,0:T(8,128)S(1)} fusion(bf16[4096,1536]{1,0:T(8,128)(2,1)} %get-tuple-element.440, f32[96,4096]{1,0:T(8,128)S(1)} %bitcast.127, f32[4096]{0:T(1024)S(1)} %bitcast.139, f32[96]{0:T(128)S(1)} %add_rsqrt_fusion.3), kind=kOutput, calls=%fused_computation.17.clone.1 | convolution fusion | flops 1209139200 | bytes 14762368 | tf_op jit(solution)/shard_map/while/body/eval_jaxpr/dot_general | solution.py:164
  358.6 4.8 convolution_convert_fusion.4
  368.0 9.4 %all-to-all-done.1 = bf16[4,96,1024]{2,1,0:T(8,128)(2,1)S(1)} async-done(((bf16[4,96,1024]{2,1,0:T(8,128)(2,1)}), bf16[4,96,1024]{2,1,0:T(8,128)(2,1)S(1)}, u32[]{:S(2)}, u32[]{:S(2)}) %all-to-all-start.1) | async-done | bytes 786464 | tf_op jit(solution)/shard_map/while/body/eval_jaxpr/all_to_all | solution.py:67
  377.7 6.9 %collective-permute-done = bf16[96,1024]{1,0:T(8,128)(2,1)S(1)} collective-permute-done((bf16[96,1024]{1,0:T(8,128)(2,1)S(1)}, bf16[96,1024]{1,0:T(8,128)(2,1)S(1)}, u32[]{:S(2)}, u32[]{:S(2)}) %collective-permute-start) | collective-permute-done | bytes 196640 | tf_op jit(solution)/shard_map/while/body/eval_jaxpr/ppermute | solution.py:74
  385.6 3.5 all-to-all-start
  390.8 7.7 %all-to-all-done = bf16[4,96,1024]{2,1,0:T(8,128)(2,1)S(1)} async-done(((bf16[4,96,1024]{2,1,0:T(8,128)(2,1)}), bf16[4,96,1024]{2,1,0:T(8,128)(2,1)S(1)}, u32[]{:S(2)}, u32[]{:S(2)}) %all-to-all-start) | async-done | bytes 786464 | tf_op jit(solution)/shard_map/while/body/eval_jaxpr/all_to_all | solution.py:52
  399.1 6.8 %fusion.84 = f32[96,1536]{1,0:T(8,128)S(1)} fusion(bf16[4096,1536]{1,0:T(8,128)(2,1)} %get-tuple-element.440, f32[96,4096]{1,0:T(8,128)S(1)} %bitcast.127, f32[4096]{0:T(1024)S(1)} %bitcast.139, f32[96]{0:T(128)S(1)} %add_rsqrt_fusion.3), kind=kOutput, calls=%fused_computation.17.clone.1 | convolution fusion | flops 1209139200 | bytes 14762368 | tf_op jit(solution)/shard_map/while/body/eval_jaxpr/dot_general | solution.py:164
  408.1 4.8 convolution_convert_fusion.4
  413.9 3.5 all-to-all-start.1
  417.5 10.7 %all-to-all-done.1 = bf16[4,96,1024]{2,1,0:T(8,128)(2,1)S(1)} async-done(((bf16[4,96,1024]{2,1,0:T(8,128)(2,1)}), bf16[4,96,1024]{2,1,0:T(8,128)(2,1)S(1)}, u32[]{:S(2)}, u32[]{:S(2)}) %all-to-all-start.1) | async-done | bytes 786464 | tf_op jit(solution)/shard_map/while/body/eval_jaxpr/all_to_all | solution.py:67
  428.4 6.9 %collective-permute-done = bf16[96,1024]{1,0:T(8,128)(2,1)S(1)} collective-permute-done((bf16[96,1024]{1,0:T(8,128)(2,1)S(1)}, bf16[96,1024]{1,0:T(8,128)(2,1)S(1)}, u32[]{:S(2)}, u32[]{:S(2)}) %collective-permute-start) | collective-permute-done | bytes 196640 | tf_op jit(solution)/shard_map/while/body/eval_jaxpr/ppermute | solution.py:74
  441.6 7.7 %all-to-all-done = bf16[4,96,1024]{2,1,0:T(8,128)(2,1)S(1)} async-done(((bf16[4,96,1024]{2,1,0:T(8,128)(2,1)}), bf16[4,96,1024]{2,1,0:T(8,128)(2,1)S(1)}, u32[]{:S(2)}, u32[]{:S(2)}) %all-to-all-start) | async-done | bytes 786464 | tf_op jit(solution)/shard_map/while/body/eval_jaxpr/all_to_all | solution.py:52
  449.8 6.8 %fusion.84 = f32[96,1536]{1,0:T(8,128)S(1)} fusion(bf16[4096,1536]{1,0:T(8,128)(2,1)} %get-tuple-element.440, f32[96,4096]{1,0:T(8,128)S(1)} %bitcast.127, f32[4096]{0:T(1024)S(1)} %bitcast.139, f32[96]{0:T(128)S(1)} %add_rsqrt_fusion.3), kind=kOutput, calls=%fused_computation.17.clone.1 | convolution fusion | flops 1209139200 | bytes 14762368 | tf_op jit(solution)/shard_map/while/body/eval_jaxpr/dot_general | solution.py:164
  458.9 4.8 convolution_convert_fusion.4
  464.7 3.5 all-to-all-start.1
  468.2 13.1 %all-to-all-done.1 = bf16[4,96,1024]{2,1,0:T(8,128)(2,1)S(1)} async-done(((bf16[4,96,1024]{2,1,0:T(8,128)(2,1)}), bf16[4,96,1024]{2,1,0:T(8,128)(2,1)S(1)}, u32[]{:S(2)}, u32[]{:S(2)}) %all-to-all-start.1) | async-done | bytes 786464 | tf_op jit(solution)/shard_map/while/body/eval_jaxpr/all_to_all | solution.py:67
  481.6 6.9 %collective-permute-done = bf16[96,1024]{1,0:T(8,128)(2,1)S(1)} collective-permute-done((bf16[96,1024]{1,0:T(8,128)(2,1)S(1)}, bf16[96,1024]{1,0:T(8,128)(2,1)S(1)}, u32[]{:S(2)}, u32[]{:S(2)}) %collective-permute-start) | collective-permute-done | bytes 196640 | tf_op jit(solution)/shard_map/while/body/eval_jaxpr/ppermute | solution.py:74
  494.8 7.7 %all-to-all-done = bf16[4,96,1024]{2,1,0:T(8,128)(2,1)S(1)} async-done(((bf16[4,96,1024]{2,1,0:T(8,128)(2,1)}), bf16[4,96,1024]{2,1,0:T(8,128)(2,1)S(1)}, u32[]{:S(2)}, u32[]{:S(2)}) %all-to-all-start) | async-done | bytes 786464 | tf_op jit(solution)/shard_map/while/body/eval_jaxpr/all_to_all | solution.py:52
  503.0 6.8 %fusion.84 = f32[96,1536]{1,0:T(8,128)S(1)} fusion(bf16[4096,1536]{1,0:T(8,128)(2,1)} %get-tuple-element.440, f32[96,4096]{1,0:T(8,128)S(1)} %bitcast.127, f32[4096]{0:T(1024)S(1)} %bitcast.139, f32[96]{0:T(128)S(1)} %add_rsqrt_fusion.3), kind=kOutput, calls=%fused_computation.17.clone.1 | convolution fusion | flops 1209139200 | bytes 14762368 | tf_op jit(solution)/shard_map/while/body/eval_jaxpr/dot_general | solution.py:164
  512.0 4.8 convolution_convert_fusion.4
  517.9 3.5 all-to-all-start.1
  521.4 10.0 %all-to-all-done.1 = bf16[4,96,1024]{2,1,0:T(8,128)(2,1)S(1)} async-done(((bf16[4,96,1024]{2,1,0:T(8,128)(2,1)}), bf16[4,96,1024]{2,1,0:T(8,128)(2,1)S(1)}, u32[]{:S(2)}, u32[]{:S(2)}) %all-to-all-start.1) | async-done | bytes 786464 | tf_op jit(solution)/shard_map/while/body/eval_jaxpr/all_to_all | solution.py:67
  531.7 6.9 %collective-permute-done = bf16[96,1024]{1,0:T(8,128)(2,1)S(1)} collective-permute-done((bf16[96,1024]{1,0:T(8,128)(2,1)S(1)}, bf16[96,1024]{1,0:T(8,128)(2,1)S(1)}, u32[]{:S(2)}, u32[]{:S(2)}) %collective-permute-start) | collective-permute-done | bytes 196640 | tf_op jit(solution)/shard_map/while/body/eval_jaxpr/ppermute | solution.py:74
  539.5 3.5 all-to-all-start
  544.8 9.5 %all-to-all-done = bf16[4,96,1024]{2,1,0:T(8,128)(2,1)S(1)} async-done(((bf16[4,96,1024]{2,1,0:T(8,128)(2,1)}), bf16[4,96,1024]{2,1,0:T(8,128)(2,1)S(1)}, u32[]{:S(2)}, u32[]{:S(2)}) %all-to-all-start) | async-done | bytes 786464 | tf_op jit(solution)/shard_map/while/body/eval_jaxpr/all_to_all | solution.py:52
  554.8 6.8 %fusion.84 = f32[96,1536]{1,0:T(8,128)S(1)} fusion(bf16[4096,1536]{1,0:T(8,128)(2,1)} %get-tuple-element.440, f32[96,4096]{1,0:T(8,128)S(1)} %bitcast.127, f32[4096]{0:T(1024)S(1)} %bitcast.139, f32[96]{0:T(128)S(1)} %add_rsqrt_fusion.3), kind=kOutput, calls=%fused_computation.17.clone.1 | convolution fusion | flops 1209139200 | bytes 14762368 | tf_op jit(solution)/shard_map/while/body/eval_jaxpr/dot_general | solution.py:164
  563.9 4.8 convolution_convert_fusion.4
  573.2 9.4 %all-to-all-done.1 = bf16[4,96,1024]{2,1,0:T(8,128)(2,1)S(1)} async-done(((bf16[4,96,1024]{2,1,0:T(8,128)(2,1)}), bf16[4,96,1024]{2,1,0:T(8,128)(2,1)S(1)}, u32[]{:S(2)}, u32[]{:S(2)}) %all-to-all-start.1) | async-done | bytes 786464 | tf_op jit(solution)/shard_map/while/body/eval_jaxpr/all_to_all | solution.py:67
  582.9 6.9 %collective-permute-done = bf16[96,1024]{1,0:T(8,128)(2,1)S(1)} collective-permute-done((bf16[96,1024]{1,0:T(8,128)(2,1)S(1)}, bf16[96,1024]{1,0:T(8,128)(2,1)S(1)}, u32[]{:S(2)}, u32[]{:S(2)}) %collective-permute-start) | collective-permute-done | bytes 196640 | tf_op jit(solution)/shard_map/while/body/eval_jaxpr/ppermute | solution.py:74
  594.5 9.2 %all-to-all-done.3 = bf16[4,96,1024]{2,1,0:T(8,128)(2,1)S(1)} async-done(((bf16[4,96,1024]{2,1,0:T(8,128)(2,1)}), bf16[4,96,1024]{2,1,0:T(8,128)(2,1)S(1)}, u32[]{:S(2)}, u32[]{:S(2)}) %all-to-all-start.3) | async-done | bytes 786464 | tf_op jit(solution)/shard_map/all_to_all | solution.py:52
  604.3 5.5 all-to-all-start.5
  611.1 6.0 all-to-all-done.5
  618.8 4.0 all-to-all-start.4
  623.5 27.6 %all-to-all-done.4 = bf16[32,32,1024]{2,1,0:T(8,128)(2,1)S(1)} async-done(((bf16[32,32,1024]{2,1,0:T(8,128)(2,1)}), bf16[32,32,1024]{2,1,0:T(8,128)(2,1)S(1)}, u32[]{:S(2)}, u32[]{:S(2)}) %all-to-all-start.4) | async-done | bytes 2097184 | tf_op jit(solution)/shard_map/all_to_all | solution.py:52
  652.1 8.9 %psum.7 = f32[1,16]{1,0:T(1,128)S(1)} all-reduce(f32[1,16]{1,0:T(1,128)S(1)} %bitcast.149), channel_id=1, replica_groups=mesh['dp'=8,'pipe'=4,'tensor'=4] {'tensor'}, use_global_device_ids=true, to_apply=%region_13.14 | all-reduce | flops 16 | bytes 128 | tf_op jit(solution)/shard_map/psum | solution.py:237
  (329 shorter events, 105.3 us)
Async XLA Ops:
  0.6 3.9 collective-permute-start.1
  5.2 5.1 collective-permute-start.2
  10.3 1.2 collective-permute-start.3
  11.6 3.7 collective-permute-start.4
  15.3 36.1 %collective-permute-start.5 = (s32[16,2,32]{2,1,0:T(2,128)S(1)}, s32[16,2,32]{2,1,0:T(2,128)S(1)}, u32[]{:S(2)}, u32[]{:S(2)}) collective-permute-start(s32[16,2,32]{2,1,0:T(2,128)S(1)} %pad_add_fusion.2), channel_id=1, source_target_pairs={{0,64},{4,68},{8,72},{12,76},{16,80},{20,84},{24,88},{28,92},{32,9... | collective-permute-start | bytes 12296 | tf_op jit(solution)/shard_map/ppermute | solution.py:29
  77.4 5.7 copy-start.5
  77.4 7.1 %copy-start.4 = (s32[2]{0:T(128)S(1)}, s32[2]{0:T(128)}, u32[]{:S(2)}) copy-start(s32[2]{0:T(128)} %param.16) | copy-start | bytes 28
  77.4 87.5 %copy-start = (bf16[1,4096,256]{2,1,0:T(8,128)(2,1)S(1)}, bf16[1,4096,256]{2,1,0:T(8,128)(2,1)}, u32[]{:S(2)}) copy-start(bf16[1,4096,256]{2,1,0:T(8,128)(2,1)} %param.25) | copy-start | bytes 6291460
  77.4 99.1 %all-to-all-start.2 = ((bf16[32,96,1024]{2,1,0:T(8,128)(2,1)}), bf16[32,96,1024]{2,1,0:T(8,128)(2,1)}, u32[]{:S(2)}, u32[]{:S(2)}) async-start(bf16[32,96,1024]{2,1,0:T(8,128)(2,1)} %select_select_fusion), calls=%async_computation.2 | async-start | bytes 12582912 | tf_op jit(solution)/shard_map/all_to_all | solution.py:143
  176.5 4.3 copy-start.1
  180.8 413.6 %copy-start.3 = (s32[2,1]{0,1:T(1,128)S(1)}, s32[2,1]{0,1:T(1,128)}, u32[]{:S(2)}) copy-start(s32[2,1]{0,1:T(1,128)} %param.17) | copy-start | bytes 28
  181.8 17.2 %all-to-all-start = ((bf16[4,96,1024]{2,1,0:T(8,128)(2,1)}), bf16[4,96,1024]{2,1,0:T(8,128)(2,1)S(1)}, u32[]{:S(2)}, u32[]{:S(2)}) async-start(bf16[4,96,1024]{2,1,0:T(8,128)(2,1)} %broadcast_in_dim.173), calls=%async_computation | async-start | bytes 1572864 | tf_op jit(solution)/shard_map/while/body/eval_jaxpr/all_to_all | solution.py:52
  214.4 14.5 %all-to-all-start.1 = ((bf16[4,96,1024]{2,1,0:T(8,128)(2,1)}), bf16[4,96,1024]{2,1,0:T(8,128)(2,1)S(1)}, u32[]{:S(2)}, u32[]{:S(2)}) async-start(bf16[4,96,1024]{2,1,0:T(8,128)(2,1)} %bitcast.124), calls=%async_computation.1 | async-start | bytes 1572864 | tf_op jit(solution)/shard_map/while/body/eval_jaxpr/all_to_all | solution.py:67
  229.1 6.9 %collective-permute-start = (bf16[96,1024]{1,0:T(8,128)(2,1)S(1)}, bf16[96,1024]{1,0:T(8,128)(2,1)S(1)}, u32[]{:S(2)}, u32[]{:S(2)}) collective-permute-start(bf16[96,1024]{1,0:T(8,128)(2,1)S(1)} %fusion.89), channel_id=1, source_target_pairs={{12,0},{0,4},{4,8},{8,12},{13,1},{1,5},{5,9},{9,13},{14,2},{2,6},{... | collective-permute-start | bytes 589832 | tf_op jit(solution)/shard_map/while/body/eval_jaxpr/ppermute | solution.py:74
  237.1 13.0 %all-to-all-start = ((bf16[4,96,1024]{2,1,0:T(8,128)(2,1)}), bf16[4,96,1024]{2,1,0:T(8,128)(2,1)S(1)}, u32[]{:S(2)}, u32[]{:S(2)}) async-start(bf16[4,96,1024]{2,1,0:T(8,128)(2,1)} %broadcast_in_dim.173), calls=%async_computation | async-start | bytes 1572864 | tf_op jit(solution)/shard_map/while/body/eval_jaxpr/all_to_all | solution.py:52
  265.5 13.0 %all-to-all-start.1 = ((bf16[4,96,1024]{2,1,0:T(8,128)(2,1)}), bf16[4,96,1024]{2,1,0:T(8,128)(2,1)S(1)}, u32[]{:S(2)}, u32[]{:S(2)}) async-start(bf16[4,96,1024]{2,1,0:T(8,128)(2,1)} %bitcast.124), calls=%async_computation.1 | async-start | bytes 1572864 | tf_op jit(solution)/shard_map/while/body/eval_jaxpr/all_to_all | solution.py:67
  278.6 6.9 %collective-permute-start = (bf16[96,1024]{1,0:T(8,128)(2,1)S(1)}, bf16[96,1024]{1,0:T(8,128)(2,1)S(1)}, u32[]{:S(2)}, u32[]{:S(2)}) collective-permute-start(bf16[96,1024]{1,0:T(8,128)(2,1)S(1)} %fusion.89), channel_id=1, source_target_pairs={{12,0},{0,4},{4,8},{8,12},{13,1},{1,5},{5,9},{9,13},{14,2},{2,6},{... | collective-permute-start | bytes 589832 | tf_op jit(solution)/shard_map/while/body/eval_jaxpr/ppermute | solution.py:74
  286.6 13.0 %all-to-all-start = ((bf16[4,96,1024]{2,1,0:T(8,128)(2,1)}), bf16[4,96,1024]{2,1,0:T(8,128)(2,1)S(1)}, u32[]{:S(2)}, u32[]{:S(2)}) async-start(bf16[4,96,1024]{2,1,0:T(8,128)(2,1)} %broadcast_in_dim.173), calls=%async_computation | async-start | bytes 1572864 | tf_op jit(solution)/shard_map/while/body/eval_jaxpr/all_to_all | solution.py:52
  314.9 13.0 %all-to-all-start.1 = ((bf16[4,96,1024]{2,1,0:T(8,128)(2,1)}), bf16[4,96,1024]{2,1,0:T(8,128)(2,1)S(1)}, u32[]{:S(2)}, u32[]{:S(2)}) async-start(bf16[4,96,1024]{2,1,0:T(8,128)(2,1)} %bitcast.124), calls=%async_computation.1 | async-start | bytes 1572864 | tf_op jit(solution)/shard_map/while/body/eval_jaxpr/all_to_all | solution.py:67
  328.1 6.9 %collective-permute-start = (bf16[96,1024]{1,0:T(8,128)(2,1)S(1)}, bf16[96,1024]{1,0:T(8,128)(2,1)S(1)}, u32[]{:S(2)}, u32[]{:S(2)}) collective-permute-start(bf16[96,1024]{1,0:T(8,128)(2,1)S(1)} %fusion.89), channel_id=1, source_target_pairs={{12,0},{0,4},{4,8},{8,12},{13,1},{1,5},{5,9},{9,13},{14,2},{2,6},{... | collective-permute-start | bytes 589832 | tf_op jit(solution)/shard_map/while/body/eval_jaxpr/ppermute | solution.py:74
  336.1 13.0 %all-to-all-start = ((bf16[4,96,1024]{2,1,0:T(8,128)(2,1)}), bf16[4,96,1024]{2,1,0:T(8,128)(2,1)S(1)}, u32[]{:S(2)}, u32[]{:S(2)}) async-start(bf16[4,96,1024]{2,1,0:T(8,128)(2,1)} %broadcast_in_dim.173), calls=%async_computation | async-start | bytes 1572864 | tf_op jit(solution)/shard_map/while/body/eval_jaxpr/all_to_all | solution.py:52
  364.4 13.0 %all-to-all-start.1 = ((bf16[4,96,1024]{2,1,0:T(8,128)(2,1)}), bf16[4,96,1024]{2,1,0:T(8,128)(2,1)S(1)}, u32[]{:S(2)}, u32[]{:S(2)}) async-start(bf16[4,96,1024]{2,1,0:T(8,128)(2,1)} %bitcast.124), calls=%async_computation.1 | async-start | bytes 1572864 | tf_op jit(solution)/shard_map/while/body/eval_jaxpr/all_to_all | solution.py:67
  377.6 6.9 %collective-permute-start = (bf16[96,1024]{1,0:T(8,128)(2,1)S(1)}, bf16[96,1024]{1,0:T(8,128)(2,1)S(1)}, u32[]{:S(2)}, u32[]{:S(2)}) collective-permute-start(bf16[96,1024]{1,0:T(8,128)(2,1)S(1)} %fusion.89), channel_id=1, source_target_pairs={{12,0},{0,4},{4,8},{8,12},{13,1},{1,5},{5,9},{9,13},{14,2},{2,6},{... | collective-permute-start | bytes 589832 | tf_op jit(solution)/shard_map/while/body/eval_jaxpr/ppermute | solution.py:74
  385.6 13.0 %all-to-all-start = ((bf16[4,96,1024]{2,1,0:T(8,128)(2,1)}), bf16[4,96,1024]{2,1,0:T(8,128)(2,1)S(1)}, u32[]{:S(2)}, u32[]{:S(2)}) async-start(bf16[4,96,1024]{2,1,0:T(8,128)(2,1)} %broadcast_in_dim.173), calls=%async_computation | async-start | bytes 1572864 | tf_op jit(solution)/shard_map/while/body/eval_jaxpr/all_to_all | solution.py:52
  413.9 14.2 %all-to-all-start.1 = ((bf16[4,96,1024]{2,1,0:T(8,128)(2,1)}), bf16[4,96,1024]{2,1,0:T(8,128)(2,1)S(1)}, u32[]{:S(2)}, u32[]{:S(2)}) async-start(bf16[4,96,1024]{2,1,0:T(8,128)(2,1)} %bitcast.124), calls=%async_computation.1 | async-start | bytes 1572864 | tf_op jit(solution)/shard_map/while/body/eval_jaxpr/all_to_all | solution.py:67
  428.4 6.9 %collective-permute-start = (bf16[96,1024]{1,0:T(8,128)(2,1)S(1)}, bf16[96,1024]{1,0:T(8,128)(2,1)S(1)}, u32[]{:S(2)}, u32[]{:S(2)}) collective-permute-start(bf16[96,1024]{1,0:T(8,128)(2,1)S(1)} %fusion.89), channel_id=1, source_target_pairs={{12,0},{0,4},{4,8},{8,12},{13,1},{1,5},{5,9},{9,13},{14,2},{2,6},{... | collective-permute-start | bytes 589832 | tf_op jit(solution)/shard_map/while/body/eval_jaxpr/ppermute | solution.py:74
  436.3 13.0 %all-to-all-start = ((bf16[4,96,1024]{2,1,0:T(8,128)(2,1)}), bf16[4,96,1024]{2,1,0:T(8,128)(2,1)S(1)}, u32[]{:S(2)}, u32[]{:S(2)}) async-start(bf16[4,96,1024]{2,1,0:T(8,128)(2,1)} %broadcast_in_dim.173), calls=%async_computation | async-start | bytes 1572864 | tf_op jit(solution)/shard_map/while/body/eval_jaxpr/all_to_all | solution.py:52
  464.7 16.6 %all-to-all-start.1 = ((bf16[4,96,1024]{2,1,0:T(8,128)(2,1)}), bf16[4,96,1024]{2,1,0:T(8,128)(2,1)S(1)}, u32[]{:S(2)}, u32[]{:S(2)}) async-start(bf16[4,96,1024]{2,1,0:T(8,128)(2,1)} %bitcast.124), calls=%async_computation.1 | async-start | bytes 1572864 | tf_op jit(solution)/shard_map/while/body/eval_jaxpr/all_to_all | solution.py:67
  481.5 6.9 %collective-permute-start = (bf16[96,1024]{1,0:T(8,128)(2,1)S(1)}, bf16[96,1024]{1,0:T(8,128)(2,1)S(1)}, u32[]{:S(2)}, u32[]{:S(2)}) collective-permute-start(bf16[96,1024]{1,0:T(8,128)(2,1)S(1)} %fusion.89), channel_id=1, source_target_pairs={{12,0},{0,4},{4,8},{8,12},{13,1},{1,5},{5,9},{9,13},{14,2},{2,6},{... | collective-permute-start | bytes 589832 | tf_op jit(solution)/shard_map/while/body/eval_jaxpr/ppermute | solution.py:74
  489.5 13.0 %all-to-all-start = ((bf16[4,96,1024]{2,1,0:T(8,128)(2,1)}), bf16[4,96,1024]{2,1,0:T(8,128)(2,1)S(1)}, u32[]{:S(2)}, u32[]{:S(2)}) async-start(bf16[4,96,1024]{2,1,0:T(8,128)(2,1)} %broadcast_in_dim.173), calls=%async_computation | async-start | bytes 1572864 | tf_op jit(solution)/shard_map/while/body/eval_jaxpr/all_to_all | solution.py:52
  517.9 13.5 %all-to-all-start.1 = ((bf16[4,96,1024]{2,1,0:T(8,128)(2,1)}), bf16[4,96,1024]{2,1,0:T(8,128)(2,1)S(1)}, u32[]{:S(2)}, u32[]{:S(2)}) async-start(bf16[4,96,1024]{2,1,0:T(8,128)(2,1)} %bitcast.124), calls=%async_computation.1 | async-start | bytes 1572864 | tf_op jit(solution)/shard_map/while/body/eval_jaxpr/all_to_all | solution.py:67
  531.6 6.9 %collective-permute-start = (bf16[96,1024]{1,0:T(8,128)(2,1)S(1)}, bf16[96,1024]{1,0:T(8,128)(2,1)S(1)}, u32[]{:S(2)}, u32[]{:S(2)}) collective-permute-start(bf16[96,1024]{1,0:T(8,128)(2,1)S(1)} %fusion.89), channel_id=1, source_target_pairs={{12,0},{0,4},{4,8},{8,12},{13,1},{1,5},{5,9},{9,13},{14,2},{2,6},{... | collective-permute-start | bytes 589832 | tf_op jit(solution)/shard_map/while/body/eval_jaxpr/ppermute | solution.py:74
  539.5 14.7 %all-to-all-start = ((bf16[4,96,1024]{2,1,0:T(8,128)(2,1)}), bf16[4,96,1024]{2,1,0:T(8,128)(2,1)S(1)}, u32[]{:S(2)}, u32[]{:S(2)}) async-start(bf16[4,96,1024]{2,1,0:T(8,128)(2,1)} %broadcast_in_dim.173), calls=%async_computation | async-start | bytes 1572864 | tf_op jit(solution)/shard_map/while/body/eval_jaxpr/all_to_all | solution.py:52
  569.7 13.0 %all-to-all-start.1 = ((bf16[4,96,1024]{2,1,0:T(8,128)(2,1)}), bf16[4,96,1024]{2,1,0:T(8,128)(2,1)S(1)}, u32[]{:S(2)}, u32[]{:S(2)}) async-start(bf16[4,96,1024]{2,1,0:T(8,128)(2,1)} %bitcast.124), calls=%async_computation.1 | async-start | bytes 1572864 | tf_op jit(solution)/shard_map/while/body/eval_jaxpr/all_to_all | solution.py:67
  582.8 6.9 %collective-permute-start = (bf16[96,1024]{1,0:T(8,128)(2,1)S(1)}, bf16[96,1024]{1,0:T(8,128)(2,1)S(1)}, u32[]{:S(2)}, u32[]{:S(2)}) collective-permute-start(bf16[96,1024]{1,0:T(8,128)(2,1)S(1)} %fusion.89), channel_id=1, source_target_pairs={{12,0},{0,4},{4,8},{8,12},{13,1},{1,5},{5,9},{9,13},{14,2},{2,6},{... | collective-permute-start | bytes 589832 | tf_op jit(solution)/shard_map/while/body/eval_jaxpr/ppermute | solution.py:74
  590.8 13.0 %all-to-all-start.3 = ((bf16[4,96,1024]{2,1,0:T(8,128)(2,1)}), bf16[4,96,1024]{2,1,0:T(8,128)(2,1)S(1)}, u32[]{:S(2)}, u32[]{:S(2)}) async-start(bf16[4,96,1024]{2,1,0:T(8,128)(2,1)} %broadcast_in_dim.132), calls=%async_computation.3 | async-start | bytes 1572864 | tf_op jit(solution)/shard_map/all_to_all | solution.py:52
  594.3 16.2 %dynamic-slice-start = ((f32[4096]{0:T(1024)}, s32[]{:T(128)}), f32[1024]{0:T(1024)S(1)}, s32[]{:S(2)}) async-start(f32[4096]{0:T(1024)} %param.27, s32[]{:T(128)} %select_n.193), calls=%async_computation.6 | async-start | bytes 8704 | tf_op jit(solution)/shard_map/dynamic_slice | solution.py:209
  604.3 12.8 %all-to-all-start.5 = ((bf16[32,1,32]{2,1,0:T(2,128)(2,1)}), bf16[32,1,32]{2,1,0:T(2,128)(2,1)S(1)}, u32[]{:S(2)}, u32[]{:S(2)}) async-start(bf16[32,1,32]{2,1,0:T(2,128)(2,1)} %broadcast_in_dim.134), calls=%async_computation.5 | async-start | bytes 32768 | tf_op jit(solution)/shard_map/all_to_all | solution.py:52
  618.8 32.3 %all-to-all-start.4 = ((bf16[32,32,1024]{2,1,0:T(8,128)(2,1)}), bf16[32,32,1024]{2,1,0:T(8,128)(2,1)S(1)}, u32[]{:S(2)}, u32[]{:S(2)}) async-start(bf16[32,32,1024]{2,1,0:T(8,128)(2,1)} %broadcast_in_dim.133), calls=%async_computation.4 | async-start | bytes 4194304 | tf_op jit(solution)/shard_map/all_to_all | solution.py:52
  651.5 10.0 %copy-start.2 = (f32[32,1024]{1,0:T(8,128)}, f32[32,1024]{1,0:T(8,128)S(1)}, u32[]{:S(2)}) copy-start(f32[32,1024]{1,0:T(8,128)S(1)} %broadcast_divide_fusion) | copy-start | bytes 393220
